TPU v7x, 512 devices: a whole 4x8x8 slice. The times are simulated.
512 devices in a mesh: dp: 64 (over y, x, core), mp: 8 (over z).
Axes of the slice: x: 4, y: 8, z: 8, core: 2. Of those that a mesh axis runs over, the one named last changes fastest.
Arguments:
- hidden: bfloat16 [960, 128, 2048], P('dp', None, 'mp'), may hold values from -6 to 6
- attn_out: bfloat16 [960, 128, 2048], P('dp', None, 'mp'), may hold values from -6 to 6
- out_proj: bfloat16 [2048, 2048], P(None, 'mp'), may hold values from -0.125 to 0.125
- norm_gain: float32 [2048], P('mp'), may hold values from 0.1 to 1.9
- reward_proj: float32 [2048, 8], P('mp'), may hold values from -0.125 to 0.125
- block_seq: int32 [960], replicated, may hold values from -1 to 383, as said below
- block_dest: int32 [960], replicated, may hold values from -1 to 639, as said below
- lengths: int32 [384], replicated, may hold values from 1 to 512, as said below
Outputs:
- token_rewards: float32 [640, 8, 128], P('dp')
- advantages: float32 [384], P('dp')
Inputs may be any that keep to these rules, and one draw needn't show every extreme that they name: `block_seq`: used slots of each index of dp come first in its 15 slots, the rest hold -1; each index of dp holds 1 to 15 used slots and some index holds exactly 15. Read over used slots in slot order, response numbers never fall, every response appears, and each has 1 to 4 blocks. `block_dest`: exactly the used slots (those of block_seq that are not -1) hold a destination; every owned slot of every owner is named exactly once, so each owner receives exactly 10 blocks; at most 1 block go from one index of dp to one owner, and that many in some pair. `lengths`: A response of n blocks has more than 128 * (n - 1) and at most 128 * n tokens.
All inputs are finite; a program needn't handle non-finite values.
Results may differ from a plain program's by a relative error of at most 0.0029.
Values may be sent and summed in bfloat16 or wider, within the bound.
No kernel may reach another device: no remote copies, remote signals or barrier semaphores. Data moves between devices by JAX's collectives and lax.ppermute only.
A program may use at most 64 MiB of HBM per device.

v0:
```python
import jax
import jax.numpy as jnp
from jax import lax
from jax.sharding import PartitionSpec as P

OWN_CAP = 10
norm_epsilon = 1e-05
stat_epsilon = 1e-06


def sent_to_all(value, axis):
    copies = jnp.broadcast_to(value, (lax.axis_size(axis), *value.shape))
    return lax.all_to_all(copies, axis, split_axis=0, concat_axis=0, tiled=True)


def of_everyone(value, axis):
    everything = sent_to_all(value, axis)
    return jnp.sum(everything, axis=0)


def packed_total(arrays, axis):
    ends = [0]
    for a in arrays:
        ends.append(ends[-1] + a.size)
    so_far = of_everyone(jnp.concatenate([a.ravel() for a in arrays]), axis)
    return tuple((so_far[b:e].reshape(a.shape) for a, b, e in zip(arrays, ends, ends[1:])))


def split_up(value, dim, peers):
    before, after = (value.shape[:dim], value.shape[dim + 1 :])
    return jnp.moveaxis(value.reshape(*before, peers, -1, *after), dim, 0)


def sent_and_summed(value, axis, dim):
    parts = split_up(value, dim, lax.axis_size(axis))
    arrived = lax.all_to_all(parts, axis, split_axis=0, concat_axis=0, tiled=True)
    return arrived.sum(axis=0)


def local(hidden, attn_out, out_proj, norm_gain, reward_proj, block_seq, block_dest, lengths):
    device_count = lax.axis_size("dp")
    device_rank = lax.axis_index("dp")
    slots_in = hidden.shape[0]
    block_len = hidden.shape[1]
    model_width = out_proj.shape[0]
    seq_count = lengths.shape[0]
    seq_local = seq_count // device_count
    slot_depth = (slots_in + device_count - 1) // device_count
    all_slots = jnp.arange(block_dest.shape[0], dtype=jnp.int32)
    local_dest = lax.dynamic_slice_in_dim(block_dest, device_rank * slots_in, slots_in)
    is_used = local_dest >= 0
    owner_rank = jnp.where(is_used, local_dest // OWN_CAP, -1)
    local_slots = jnp.arange(slots_in, dtype=jnp.int32)
    earlier = (
        (owner_rank[None, :] == owner_rank[:, None])
        & (local_slots[None, :] < local_slots[:, None])
        & is_used[None, :]
    )
    send_row = jnp.where(is_used, owner_rank * slot_depth + earlier.sum(axis=1), -1)
    buffer_rows = jnp.arange(device_count * slot_depth, dtype=jnp.int32)
    selector = (send_row[None, :] == buffer_rows[:, None]).astype(jnp.bfloat16)
    targets = device_rank * OWN_CAP + jnp.arange(OWN_CAP, dtype=jnp.int32)
    matches = block_dest[None, :] == targets[:, None]
    source_slot = jnp.sum(jnp.where(matches, all_slots[None, :], 0), axis=1)
    source_rank = source_slot // slots_in
    before = (block_dest[None, :] >= 0) & (block_dest[None, :] // OWN_CAP == device_rank)
    before = (
        before
        & (all_slots[None, :] >= (source_rank * slots_in)[:, None])
        & (all_slots[None, :] < source_slot[:, None])
    )
    recv_row = source_rank * slot_depth + before.sum(axis=1)
    seq_own = jnp.sum(jnp.where(matches, block_seq[None, :], 0), axis=1)
    earlier_same = (block_seq[None, :] == seq_own[:, None]) & (
        all_slots[None, :] < source_slot[:, None]
    )
    seq_rank = earlier_same.sum(axis=1)
    seq_ids = jnp.arange(seq_count, dtype=jnp.int32)
    member = seq_ids[:, None] == seq_own[None, :]
    own_length = jnp.sum(jnp.where(member, lengths[:, None], 0), axis=0)
    valid_tokens = jnp.minimum(block_len, own_length - block_len * seq_rank)
    projected = jnp.einsum(
        "btf,fc->btc",
        lax.all_gather(attn_out, "mp", axis=2, tiled=True),
        out_proj,
        preferred_element_type=jnp.float32,
    )
    local_resid = (hidden.astype(jnp.float32) + projected).astype(jnp.bfloat16)
    moved_resid = lax.all_to_all(
        jnp.einsum("rj,jtf->rtf", selector, local_resid, preferred_element_type=jnp.float32).astype(
            jnp.bfloat16
        ),
        "dp",
        split_axis=0,
        concat_axis=0,
        tiled=True,
    )
    residual = jnp.take(moved_resid, recv_row, axis=0)
    values = residual.astype(jnp.float32)
    squares = jnp.sum(values * values, axis=2)
    weighted = norm_gain[:, None] * reward_proj
    partial_value = jnp.einsum("btf,fh->bht", values, weighted, precision=lax.Precision.HIGHEST)
    squares, partial_value = packed_total((squares, partial_value), "mp")
    inverse_rms = lax.rsqrt(squares / model_width + norm_epsilon)
    live_tokens = (jnp.arange(block_len, dtype=jnp.int32)[None, :] < valid_tokens[:, None]).astype(
        jnp.float32
    )
    token_rewards = partial_value * (inverse_rms * live_tokens)[:, None, :]
    block_sums = jnp.sum(token_rewards, axis=2)
    seq_part = jnp.dot(member.astype(jnp.float32), block_sums, precision=lax.Precision.HIGHEST)
    seq_totals = sent_and_summed(seq_part, "dp", 0)
    own_lengths = lax.dynamic_slice_in_dim(lengths, device_rank * seq_local, seq_local).astype(
        jnp.float32
    )
    scores = seq_totals / own_lengths[:, None]
    worst_case = jnp.min(scores, axis=1)
    head_mean = jnp.mean(scores, axis=1)
    spread = jnp.mean((scores - head_mean[:, None]) ** 2, axis=1)
    total_seqs = float(seq_count)
    moment_sums = packed_total(
        (
            jnp.sum(spread),
            jnp.sum(worst_case),
            jnp.sum(worst_case * worst_case),
            jnp.sum(worst_case * spread),
            jnp.sum(spread * spread),
        ),
        "dp",
    )
    penalty_scale = moment_sums[0] / total_seqs + stat_epsilon
    conservative = worst_case - spread / penalty_scale
    first_sum = moment_sums[1] - moment_sums[0] / penalty_scale
    second = (
        moment_sums[2]
        - 2.0 * moment_sums[3] / penalty_scale
        + moment_sums[4] / (penalty_scale * penalty_scale)
    )
    centre = first_sum / total_seqs
    variance = second / total_seqs - centre * centre
    advantages = (conservative - centre) * lax.rsqrt(variance + stat_epsilon)
    return (token_rewards, advantages)


def solution(mesh):
    return jax.shard_map(
        local,
        mesh=mesh,
        in_specs=(
            P("dp", None, "mp"),
            P("dp", None, "mp"),
            P(None, "mp"),
            P("mp"),
            P("mp", None),
            P(),
            P(),
            P(),
        ),
        out_specs=(P("dp", None, None), P("dp")),
        check_vma=False,
    )
```

profile of v0, /device:TPU:1, one launch (start us, length us, event | category | flops | bytes accessed | tf_op | source)
XLA Modules:
  0.0 305.1 jit_solution(17338030331236136521)
XLA Ops:
  7.2 0.0 copy-start
  7.2 0.0 all-gather.2.cloned.1.call-start
  7.2 0.7 all-gather.2.cloned.1.call-update
  7.9 0.8 fusion.29
  8.7 0.2 convert_reduce_fusion.2
  8.9 101.2 %all-gather.2.cloned.1.call-done = bf16[15,128,2048]{2,1,0:T(8,128)(2,1)} async-done(((bf16[15,128,256]{2,1,0:T(8,128)(2,1)}), bf16[15,128,2048]{2,1,0:T(8,128)(2,1)}) %all-gather.2.cloned.1.call-update) | async-done | bytes 7864336 | tf_op jit(solution)/shard_map/all_gather | solution.py:84
  110.1 0.0 copy-done
  110.1 5.7 %add_convert_fusion = bf16[15,128,256]{2,1,0:T(8,128)(2,1)S(1)} fusion(bf16[15,128,256]{2,1,0:T(8,128)(2,1)} %param.8, bf16[15,128,2048]{2,1,0:T(8,128)(2,1)} %all-gather.2.cloned.1.call-done, bf16[2048,256]{1,0:T(8,128)(2,1)S(1)} %copy-done), kind=kOutput, calls=%fused_computation.3 | convolution fusion | flops 2014740480 | bytes 10878976 | tf_op jit(solution)/shard_map/btf,fc->btc/dot_general | solution.py:82
  115.8 1.4 convolution_convert_fusion
  117.1 4.4 %copy.29 = bf16[64,128,256]{2,1,0:T(8,128)(2,1)} copy(bf16[64,128,256]{2,0,1:T(8,128)(2,1)S(1)} %convolution_convert_fusion) | data formatting | bytes 8388608 | tf_op jit(solution)/shard_map/convert_element_type | solution.py:90
  121.5 0.0 copy-start.1
  121.5 0.0 copy-start.2
  121.5 0.0 copy-start.4
  121.5 0.0 copy-start.5
  121.5 13.3 %all-to-all-start = ((bf16[64,128,256]{2,1,0:T(8,128)(2,1)}), bf16[64,128,256]{2,1,0:T(8,128)(2,1)}, u32[]{:S(2)}, u32[]{:S(2)}) async-start(bf16[64,128,256]{2,1,0:T(8,128)(2,1)} %copy.29), calls=%async_computation | async-start | bytes 8388608 | tf_op jit(solution)/shard_map/all_to_all | solution.py:89
  134.8 0.0 copy-start.3
  134.9 0.0 copy-done.1
  134.9 0.0 copy-done.2
  134.9 0.2 fusion.3
  135.1 0.2 convert_reduce_fusion
  135.4 94.2 %all-to-all-done = bf16[64,128,256]{2,1,0:T(8,128)(2,1)} async-done(((bf16[64,128,256]{2,1,0:T(8,128)(2,1)}), bf16[64,128,256]{2,1,0:T(8,128)(2,1)}, u32[]{:S(2)}, u32[]{:S(2)}) %all-to-all-start) | async-done | bytes 4194336 | tf_op jit(solution)/shard_map/all_to_all | solution.py:89
  229.5 2.8 gather_fusion
  232.3 0.3 multiply_reduce_fusion
  232.7 0.0 copy-done.4
  232.7 0.0 copy-done.5
  232.7 0.7 convolution_bitcast_fusion
  233.4 0.9 broadcast_in_dim.89
  234.3 3.9 %all-to-all-start.1 = ((f32[8,1,11520]{2,1,0:T(1,128)}), f32[8,1,11520]{2,1,0:T(1,128)S(1)}, u32[]{:S(2)}, u32[]{:S(2)}) async-start(f32[8,1,11520]{2,1,0:T(1,128)} %broadcast_in_dim.89), calls=%async_computation.1 | async-start | bytes 737280 | tf_op jit(solution)/shard_map/all_to_all | solution.py:13
  238.2 0.0 copy-done.3
  238.2 0.2 select_reduce_fusion
  238.4 11.5 %all-to-all-done.1 = f32[8,1,11520]{2,1,0:T(1,128)S(1)} async-done(((f32[8,1,11520]{2,1,0:T(1,128)}), f32[8,1,11520]{2,1,0:T(1,128)S(1)}, u32[]{:S(2)}, u32[]{:S(2)}) %all-to-all-start.1) | async-done | bytes 368672 | tf_op jit(solution)/shard_map/all_to_all | solution.py:13
  249.9 0.3 reduce_sum.169
  250.2 0.1 fusion.15
  250.2 0.6 fusion.34
  250.9 0.2 fusion.7
  251.1 0.8 copy.32
  251.9 9.6 %all-to-all-start.2 = ((f32[64,6,8]{2,1,0:T(8,128)}), f32[64,6,8]{2,1,0:T(8,128)S(1)}, u32[]{:S(2)}, u32[]{:S(2)}) async-start(f32[64,6,8]{2,1,0:T(8,128)} %copy.32), calls=%async_computation.2 | async-start | bytes 524288 | tf_op jit(solution)/shard_map/all_to_all | solution.py:36
  261.6 0.1 dynamic-slice_convert_fusion
  261.6 13.0 %all-to-all-done.2 = f32[64,6,8]{2,1,0:T(8,128)S(1)} async-done(((f32[64,6,8]{2,1,0:T(8,128)}), f32[64,6,8]{2,1,0:T(8,128)S(1)}, u32[]{:S(2)}, u32[]{:S(2)}) %all-to-all-start.2) | async-done | bytes 12320 | tf_op jit(solution)/shard_map/all_to_all | solution.py:36
  274.6 0.1 reduce_sum.174
  274.7 0.2 fusion.32
  274.9 0.2 multiply_reduce_fusion.1
  275.1 0.7 multiply_reduce_fusion.2
  275.8 3.2 %concatenate.7 = f32[5]{0:T(128)S(1)} concatenate(f32[1]{0:T(128)} %bitcast.13, f32[1]{0:T(128)} %bitcast.14, f32[1]{0:T(128)} %bitcast.15, f32[1]{0:T(128)} %bitcast.16, f32[1]{0:T(128)} %bitcast.17), dimensions={0} | concatenate | bytes 40 | tf_op jit(solution)/shard_map/concatenate | solution.py:25
  279.1 14.0 %all_to_all.22 = f32[64,1,5]{2,1,0:T(1,128)S(1)} all-to-all(f32[64,1,5]{2,1,0:T(1,128)S(1)} %broadcast_in_dim.93), channel_id=1, replica_groups=mesh['dp'=64,'mp'=8] {'dp'}, dimensions={0} | all-to-all | bytes 2560 | tf_op jit(solution)/shard_map/all_to_all | solution.py:13
  293.1 0.1 reduce_sum.182
  293.1 0.7 fusion.36
  297.7 0.5 subtract_multiply_fusion
  (12 shorter events, 0.1 us)
Async XLA Ops:
  7.2 102.9 %copy-start = (bf16[2048,256]{1,0:T(8,128)(2,1)S(1)}, bf16[2048,256]{1,0:T(8,128)(2,1)}, u32[]{:S(2)}) copy-start(bf16[2048,256]{1,0:T(8,128)(2,1)} %param.10) | copy-start | bytes 3145732
  7.2 102.9 %all-gather.2.cloned.1.call-start = ((), (), s32[]{:S(2)}) async-start(), calls=%async_computation.4 | async-start | bytes 8847360 | tf_op jit(solution)/shard_map/all_gather | solution.py:84
  121.5 13.3 %copy-start.1 = (s32[960]{0:T(1024)S(1)}, s32[960]{0:T(1024)}, u32[]{:S(2)}) copy-start(s32[960]{0:T(1024)} %param.14) | copy-start | bytes 11524
  121.5 13.3 %copy-start.2 = (s32[960]{0:T(1024)S(1)}, s32[960]{0:T(1024)}, u32[]{:S(2)}) copy-start(s32[960]{0:T(1024)} %param.13) | copy-start | bytes 11524
  121.5 111.1 %copy-start.4 = (f32[256,8]{0,1:T(8,128)S(1)}, f32[256,8]{0,1:T(8,128)}, u32[]{:S(2)}) copy-start(f32[256,8]{0,1:T(8,128)} %param.12) | copy-start | bytes 24580
  121.5 111.1 %copy-start.5 = (f32[256]{0:T(256)S(1)}, f32[256]{0:T(256)}, u32[]{:S(2)}) copy-start(f32[256]{0:T(256)} %param.11) | copy-start | bytes 3076
  121.5 108.0 %all-to-all-start = ((bf16[64,128,256]{2,1,0:T(8,128)(2,1)}), bf16[64,128,256]{2,1,0:T(8,128)(2,1)}, u32[]{:S(2)}, u32[]{:S(2)}) async-start(bf16[64,128,256]{2,1,0:T(8,128)(2,1)} %copy.29), calls=%async_computation | async-start | bytes 8388608 | tf_op jit(solution)/shard_map/all_to_all | solution.py:89
  134.8 103.4 %copy-start.3 = (s32[384]{0:T(512)S(1)}, s32[384]{0:T(512)}, u32[]{:S(2)}) copy-start(s32[384]{0:T(512)} %param.15) | copy-start | bytes 4612
  234.3 15.6 %all-to-all-start.1 = ((f32[8,1,11520]{2,1,0:T(1,128)}), f32[8,1,11520]{2,1,0:T(1,128)S(1)}, u32[]{:S(2)}, u32[]{:S(2)}) async-start(f32[8,1,11520]{2,1,0:T(1,128)} %broadcast_in_dim.89), calls=%async_computation.1 | async-start | bytes 737280 | tf_op jit(solution)/shard_map/all_to_all | solution.py:13
  251.9 22.7 %all-to-all-start.2 = ((f32[64,6,8]{2,1,0:T(8,128)}), f32[64,6,8]{2,1,0:T(8,128)S(1)}, u32[]{:S(2)}, u32[]{:S(2)}) async-start(f32[64,6,8]{2,1,0:T(8,128)} %copy.32), calls=%async_computation.2 | async-start | bytes 524288 | tf_op jit(solution)/shard_map/all_to_all | solution.py:36
Sparse Core Ops, SparseCore 0:
  10.0 100.0 all-gather.1
where the time goes:
time: 306 us; the launch traced here: 305 us
  waiting for transfers between devices  221 us (72%)
  starting transfers between devices  26.8 us (9%)
  between operations  18.1 us (6%)
  blocking collectives  14 us (5%)
  local copies, waits for them, and re-layouts  12.9 us (4%)
  matrix products  7.93 us (3%)
  other arithmetic  4.83 us (2%)
    all_gather x1, waiting for transfers between devices, local(): lax.all_gather(attn_out, 'mp', axis=2, tiled=True)  101 us
    all_to_all x1, waiting for transfers between devices, local(): lax.all_to_all(jnp.einsum('rj,jtf->rtf', selector, local_resid, preferred...  94.2 us
    all_to_all x1, blocking collectives, sent_to_all(): return lax.all_to_all(copies, axis, split_axis=0, concat_axis=0, tiled=True)  14 us
    all_to_all x1, starting transfers between devices, local(): lax.all_to_all(jnp.einsum('rj,jtf->rtf', selector, local_resid, preferred...  13.3 us
    all_to_all x1, waiting for transfers between devices, sent_and_summed(): lax.all_to_all(parts, axis, split_axis=0, concat_axis=0, tiled=True)  13 us
    all_to_all x1, waiting for transfers between devices, sent_to_all(): return lax.all_to_all(copies, axis, split_axis=0, concat_axis=0, tiled=True)  11.5 us
    all_to_all x1, starting transfers between devices, sent_and_summed(): lax.all_to_all(parts, axis, split_axis=0, concat_axis=0, tiled=True)  9.64 us
  transfers between devices with their start and end apart: 4, of which 4 were waited for; matrix products, arithmetic and copies ran while one was open for 1% of the time, Pallas kernels for 0%

commit v1 on v0

--- a/solution.py
+++ b/solution.py
@@ -6,6 +6,28 @@
 OWN_CAP = 10
 norm_epsilon = 1e-05
 stat_epsilon = 1e-06
+
+
+def in_order(blocks, dim):
+    lengths = list(blocks.shape[1:])
+    lengths[dim] *= blocks.shape[0]
+    return jnp.moveaxis(blocks, 0, dim).reshape(lengths)
+
+
+def ring_gather(array, axis, dim):
+    count = lax.axis_size(axis)
+    pairs = [(i, (i + 1) % count) for i in range(count)]
+    back = [(b, a) for a, b in pairs]
+    lower, upper = ([], [])
+    for hop in range(count - 1):
+        if hop % 2 == 0:
+            lower.append(lax.ppermute(lower[-1] if lower else array, axis, pairs))
+        else:
+            upper.append(lax.ppermute(upper[-1] if upper else array, axis, back))
+    pieces = jnp.stack([*lower[::-1], array, *upper])
+    shift = lax.axis_index(axis) - len(lower)
+    pieces = pieces[(jnp.arange(count) - shift) % count]
+    return in_order(pieces, dim)
 
 
 def sent_to_all(value, axis):
@@ -80,10 +102,7 @@
     own_length = jnp.sum(jnp.where(member, lengths[:, None], 0), axis=0)
     valid_tokens = jnp.minimum(block_len, own_length - block_len * seq_rank)
     projected = jnp.einsum(
-        "btf,fc->btc",
-        lax.all_gather(attn_out, "mp", axis=2, tiled=True),
-        out_proj,
-        preferred_element_type=jnp.float32,
+        "btf,fc->btc", ring_gather(attn_out, "mp", 2), out_proj, preferred_element_type=jnp.float32
     )
     local_resid = (hidden.astype(jnp.float32) + projected).astype(jnp.bfloat16)
     moved_resid = lax.all_to_all(

time: 306 us -> 331 us (1.082)
  local copies, waits for them, and re-layouts: 12.9 us -> 46.7 us
  starting transfers between devices: 26.8 us -> 51.6 us
  waiting for transfers between devices: 221 us -> 200 us
  between operations: 18.1 us -> 4.82 us
    all_gather x1 -> x0, waiting for transfers between devices: 101 us -> none  [local(): lax.all_gather(attn_out, 'mp', axis=2, tiled=True)]
    ppermute x0 -> x7, waiting for transfers between devices: none -> 81.1 us  [the longest x4 81.1 us: ring_gather(): lower.append(lax.ppermute(lower[-1] if lower else array, axis, pairs))]
    ppermute x0 -> x7, starting transfers between devices: none -> 24.4 us  [the longest x3 13.7 us: ring_gather(): upper.append(lax.ppermute(upper[-1] if upper else array, axis, back))]
    unnamed x12 -> x25, local copies, waits for them, and re-layouts: 0.03 us -> 14.4 us
    transpose x0 -> x1, local copies, waits for them, and re-layouts: none -> 10.7 us  [in_order(): return jnp.moveaxis(blocks, 0, dim).reshape(lengths)]
    gather x0 -> x1, local copies, waits for them, and re-layouts: none -> 7.8 us  [ring_gather(): pieces = pieces[(jnp.arange(count) - shift) % count]]
  transfers between devices with their start and end apart: 4 -> 10, of which waited for: 4 -> 7; matrix products, arithmetic and copies ran while one was open for 1% -> 5% of each run, Pallas kernels for 0% -> 0%
where the time goes in v1:
time: 331 us; the launch traced here: 330 us
  waiting for transfers between devices  200 us (60%)
  starting transfers between devices  51.6 us (16%)
  local copies, waits for them, and re-layouts  46.7 us (14%)
  blocking collectives  14 us (4%)
  matrix products  7.76 us (2%)
  other arithmetic  4.85 us (1%)
  between operations  4.82 us (1%)
    all_to_all x1, waiting for transfers between devices, local(): lax.all_to_all(jnp.einsum('rj,jtf->rtf', selector, local_resid, preferred...  94.2 us
    ppermute x4, waiting for transfers between devices, ring_gather(): lower.append(lax.ppermute(lower[-1] if lower else array, axis, pairs))  81.1 us
    unnamed x25, local copies, waits for them, and re-layouts  14.4 us
    all_to_all x1, starting transfers between devices, local(): lax.all_to_all(jnp.einsum('rj,jtf->rtf', selector, local_resid, preferred...  14.3 us
    all_to_all x1, blocking collectives, sent_to_all(): return lax.all_to_all(copies, axis, split_axis=0, concat_axis=0, tiled=True)  14 us
    ppermute x3, starting transfers between devices, ring_gather(): upper.append(lax.ppermute(upper[-1] if upper else array, axis, back))  13.7 us
    all_to_all x1, waiting for transfers between devices, sent_and_summed(): lax.all_to_all(parts, axis, split_axis=0, concat_axis=0, tiled=True)  13 us
    all_to_all x1, waiting for transfers between devices, sent_to_all(): return lax.all_to_all(copies, axis, split_axis=0, concat_axis=0, tiled=True)  11.6 us
  transfers between devices with their start and end apart: 10, of which 7 were waited for; matrix products, arithmetic and copies ran while one was open for 5% of the time, Pallas kernels for 0%

profile of v1, /device:TPU:1, one launch (start us, length us, event | category | flops | bytes accessed | tf_op | source)
XLA Modules:
  0.0 329.6 jit_solution(14798518004675377240)
XLA Ops:
  0.6 0.0 copy-start
  0.7 4.9 %collective-permute-start = (bf16[15,128,256]{2,1,0:T(8,128)(2,1)}, bf16[15,128,256]{2,1,0:T(8,128)(2,1)S(1)}, u32[]{:S(2)}, u32[]{:S(2)}) collective-permute-start(bf16[15,128,256]{2,1,0:T(8,128)(2,1)} %param.9), channel_id=1, source_target_pairs={{0,1},{1,2},{2,3},{3,4},{4,5},{5,6},{6,7},{7,0},{8,9},{9,10},{10,1... | collective-permute-start | bytes 2949128 | tf_op jit(solution)/shard_map/ppermute | solution.py:24
  5.6 28.3 %collective-permute-done = bf16[15,128,256]{2,1,0:T(8,128)(2,1)S(1)} collective-permute-done((bf16[15,128,256]{2,1,0:T(8,128)(2,1)}, bf16[15,128,256]{2,1,0:T(8,128)(2,1)S(1)}, u32[]{:S(2)}, u32[]{:S(2)}) %collective-permute-start) | collective-permute-done | bytes 983072 | tf_op jit(solution)/shard_map/ppermute | solution.py:24
  33.9 1.9 collective-permute-start.1
  35.9 4.6 %collective-permute-start.4 = (bf16[15,128,256]{2,1,0:T(8,128)(2,1)}, bf16[15,128,256]{2,1,0:T(8,128)(2,1)}, u32[]{:S(2)}, u32[]{:S(2)}) collective-permute-start(bf16[15,128,256]{2,1,0:T(8,128)(2,1)} %param.9), channel_id=1, source_target_pairs={{1,0},{2,1},{3,2},{4,3},{5,4},{6,5},{7,6},{0,7},{9,8},{10,9},{11,1... | collective-permute-start | bytes 2949128 | tf_op jit(solution)/shard_map/ppermute | solution.py:26
  40.4 18.7 %collective-permute-done.1 = bf16[15,128,256]{2,1,0:T(8,128)(2,1)S(1)} collective-permute-done((bf16[15,128,256]{2,1,0:T(8,128)(2,1)S(1)}, bf16[15,128,256]{2,1,0:T(8,128)(2,1)S(1)}, u32[]{:S(2)}, u32[]{:S(2)}) %collective-permute-start.1) | collective-permute-done | bytes 983072 | tf_op jit(solution)/shard_map/ppermute | solution.py:24
  59.1 1.0 copy-done.3
  60.1 1.9 collective-permute-start.2
  62.0 0.0 collective-permute-done.4
  62.0 4.6 %collective-permute-start.5 = (bf16[15,128,256]{2,1,0:T(8,128)(2,1)}, bf16[15,128,256]{2,1,0:T(8,128)(2,1)}, u32[]{:S(2)}, u32[]{:S(2)}) collective-permute-start(bf16[15,128,256]{2,1,0:T(8,128)(2,1)} %collective-permute-done.4), channel_id=1, source_target_pairs={{1,0},{2,1},{3,2},{4,3},{5,4},{6,5},{7,6},{0,7},{9,8},{10,9},{11,1... | collective-permute-start | bytes 2949128 | tf_op jit(solution)/shard_map/ppermute | solution.py:26
  66.6 17.9 %collective-permute-done.2 = bf16[15,128,256]{2,1,0:T(8,128)(2,1)} collective-permute-done((bf16[15,128,256]{2,1,0:T(8,128)(2,1)S(1)}, bf16[15,128,256]{2,1,0:T(8,128)(2,1)}, u32[]{:S(2)}, u32[]{:S(2)}) %collective-permute-start.2) | collective-permute-done | bytes 983072 | tf_op jit(solution)/shard_map/ppermute | solution.py:24
  84.5 1.9 collective-permute-start.3
  86.4 0.8 fusion.31
  87.2 0.2 convert_reduce_fusion.2
  87.4 0.0 collective-permute-done.5
  87.4 4.6 %collective-permute-start.6 = (bf16[15,128,256]{2,1,0:T(8,128)(2,1)}, bf16[15,128,256]{2,1,0:T(8,128)(2,1)S(1)}, u32[]{:S(2)}, u32[]{:S(2)}) collective-permute-start(bf16[15,128,256]{2,1,0:T(8,128)(2,1)} %collective-permute-done.5), channel_id=1, source_target_pairs={{1,0},{2,1},{3,2},{4,3},{5,4},{6,5},{7,6},{0,7},{9,8},{10,9},{11,1... | collective-permute-start | bytes 2949128 | tf_op jit(solution)/shard_map/ppermute | solution.py:26
  92.0 16.3 %collective-permute-done.3 = bf16[15,128,256]{2,1,0:T(8,128)(2,1)} collective-permute-done((bf16[15,128,256]{2,1,0:T(8,128)(2,1)}, bf16[15,128,256]{2,1,0:T(8,128)(2,1)}, u32[]{:S(2)}, u32[]{:S(2)}) %collective-permute-start.3) | collective-permute-done | bytes 983072 | tf_op jit(solution)/shard_map/ppermute | solution.py:24
  108.2 2.2 bitcast_dynamic-update-slice_fusion.7
  110.5 2.3 bitcast_dynamic-update-slice_fusion.6
  112.7 2.3 bitcast_dynamic-update-slice_fusion.5
  115.0 1.0 bitcast_dynamic-update-slice_fusion.4
  116.0 1.0 bitcast_dynamic-update-slice_fusion.3
  117.0 2.3 bitcast_dynamic-update-slice_fusion.2
  119.3 2.3 bitcast_dynamic-update-slice_fusion.1
  121.6 0.0 collective-permute-done.6
  121.6 1.0 bitcast_dynamic-update-slice_fusion
  122.6 7.8 %gather_fusion = bf16[8,15,128,256]{3,2,1,0:T(8,128)(2,1)} fusion(bf16[8,15,128,256]{3,2,1,0:T(8,128)(2,1)} %bitcast_dynamic-update-slice_fusion, s32[1024]{0:T(1024)S(1)} %pad_clamp_fusion.1), kind=kCustom, calls=%fused_computation | custom fusion | bytes 15728672 | tf_op jit(solution)/shard_map/gather | solution.py:29
  130.4 10.7 %copy.38 = bf16[15,128,8,256]{1,3,2,0:T(8,128)(2,1)} copy(bf16[15,128,8,256]{3,1,0,2:T(8,128)(2,1)} %bitcast.74) | data formatting | bytes 15728640 | tf_op jit(solution)/shard_map/transpose | solution.py:14
  141.1 0.0 copy-done
  141.1 5.5 %add_convert_fusion = bf16[15,128,256]{2,1,0:T(8,128)(2,1)S(1)} fusion(bf16[15,128,256]{2,1,0:T(8,128)(2,1)S(1)} %copy-done.1, bf16[15,128,2048]{1,2,0:T(8,128)(2,1)} %bitcast.73, bf16[2048,256]{1,0:T(8,128)(2,1)S(1)} %copy-done), kind=kOutput, calls=%fused_computation.4 | convolution fusion | flops 2014740480 | bytes 10878976 | tf_op jit(solution)/shard_map/btf,fc->btc/dot_general | solution.py:104
  146.6 1.4 convolution_convert_fusion
  148.0 0.0 copy-start.4
  148.0 0.0 copy-start.5
  148.0 0.0 copy-start.7
  148.0 0.0 copy-start.8
  148.0 4.4 %copy.41 = bf16[64,128,256]{2,1,0:T(8,128)(2,1)} copy(bf16[64,128,256]{2,0,1:T(8,128)(2,1)S(1)} %convolution_convert_fusion) | data formatting | bytes 8388608 | tf_op jit(solution)/shard_map/convert_element_type | solution.py:109
  152.4 14.3 %all-to-all-start = ((bf16[64,128,256]{2,1,0:T(8,128)(2,1)}), bf16[64,128,256]{2,1,0:T(8,128)(2,1)}, u32[]{:S(2)}, u32[]{:S(2)}) async-start(bf16[64,128,256]{2,1,0:T(8,128)(2,1)} %copy.41), calls=%async_computation | async-start | bytes 8388608 | tf_op jit(solution)/shard_map/all_to_all | solution.py:108
  166.7 0.2 fusion.3
  167.0 0.2 convert_reduce_fusion
  167.2 94.2 %all-to-all-done = bf16[64,128,256]{2,1,0:T(8,128)(2,1)} async-done(((bf16[64,128,256]{2,1,0:T(8,128)(2,1)}), bf16[64,128,256]{2,1,0:T(8,128)(2,1)}, u32[]{:S(2)}, u32[]{:S(2)}) %all-to-all-start) | async-done | bytes 4194336 | tf_op jit(solution)/shard_map/all_to_all | solution.py:108
  261.4 2.8 gather_fusion.1
  264.2 0.3 multiply_reduce_fusion
  264.5 0.7 convolution_bitcast_fusion
  265.3 0.9 broadcast_in_dim.90
  266.2 3.4 %all-to-all-start.1 = ((f32[8,1,11520]{2,1,0:T(1,128)}), f32[8,1,11520]{2,1,0:T(1,128)S(1)}, u32[]{:S(2)}, u32[]{:S(2)}) async-start(f32[8,1,11520]{2,1,0:T(1,128)} %broadcast_in_dim.90), calls=%async_computation.1 | async-start | bytes 737280 | tf_op jit(solution)/shard_map/all_to_all | solution.py:35
  269.7 0.2 select_reduce_fusion
  269.9 11.6 %all-to-all-done.1 = f32[8,1,11520]{2,1,0:T(1,128)S(1)} async-done(((f32[8,1,11520]{2,1,0:T(1,128)}), f32[8,1,11520]{2,1,0:T(1,128)S(1)}, u32[]{:S(2)}, u32[]{:S(2)}) %all-to-all-start.1) | async-done | bytes 368672 | tf_op jit(solution)/shard_map/all_to_all | solution.py:35
  281.4 0.3 reduce_sum.169
  281.7 0.1 fusion.15
  281.8 0.6 fusion.36
  282.4 0.2 fusion.7
  282.6 0.8 copy.44
  283.4 9.5 %all-to-all-start.2 = ((f32[64,6,8]{2,1,0:T(8,128)}), f32[64,6,8]{2,1,0:T(8,128)S(1)}, u32[]{:S(2)}, u32[]{:S(2)}) async-start(f32[64,6,8]{2,1,0:T(8,128)} %copy.44), calls=%async_computation.2 | async-start | bytes 524288 | tf_op jit(solution)/shard_map/all_to_all | solution.py:58
  292.9 0.1 dynamic-slice_convert_fusion
  293.0 13.0 %all-to-all-done.2 = f32[64,6,8]{2,1,0:T(8,128)S(1)} async-done(((f32[64,6,8]{2,1,0:T(8,128)}), f32[64,6,8]{2,1,0:T(8,128)S(1)}, u32[]{:S(2)}, u32[]{:S(2)}) %all-to-all-start.2) | async-done | bytes 12320 | tf_op jit(solution)/shard_map/all_to_all | solution.py:58
  306.0 0.1 reduce_sum.174
  306.1 0.2 fusion.34
  306.2 0.2 multiply_reduce_fusion.1
  306.5 0.7 multiply_reduce_fusion.2
  307.2 3.2 concatenate.7
  310.4 14.0 %all_to_all.22 = f32[64,1,5]{2,1,0:T(1,128)S(1)} all-to-all(f32[64,1,5]{2,1,0:T(1,128)S(1)} %broadcast_in_dim.94), channel_id=1, replica_groups=mesh['dp'=64,'mp'=8] {'dp'}, dimensions={0} | all-to-all | bytes 2560 | tf_op jit(solution)/shard_map/all_to_all | solution.py:35
  324.4 0.1 reduce_sum.182
  324.5 0.7 fusion.38
  329.1 0.5 subtract_multiply_fusion
  (25 shorter events, 0.2 us)
Async XLA Ops:
  0.6 140.5 %copy-start = (bf16[2048,256]{1,0:T(8,128)(2,1)S(1)}, bf16[2048,256]{1,0:T(8,128)(2,1)}, u32[]{:S(2)}) copy-start(bf16[2048,256]{1,0:T(8,128)(2,1)} %param.10) | copy-start | bytes 3145732
  0.6 115.4 %copy-start.2 = (bf16[15,128,256]{2,1,0:T(8,128)(2,1)S(1)}, bf16[15,128,256]{2,1,0:T(8,128)(2,1)}, u32[]{:S(2)}) copy-start(bf16[15,128,256]{2,1,0:T(8,128)(2,1)} %param.9) | copy-start | bytes 2949124
  0.7 33.3 %collective-permute-start = (bf16[15,128,256]{2,1,0:T(8,128)(2,1)}, bf16[15,128,256]{2,1,0:T(8,128)(2,1)S(1)}, u32[]{:S(2)}, u32[]{:S(2)}) collective-permute-start(bf16[15,128,256]{2,1,0:T(8,128)(2,1)} %param.9), channel_id=1, source_target_pairs={{0,1},{1,2},{2,3},{3,4},{4,5},{5,6},{6,7},{7,0},{8,9},{9,10},{10,1... | collective-permute-start | bytes 2949128 | tf_op jit(solution)/shard_map/ppermute | solution.py:24
  33.9 25.2 %collective-permute-start.1 = (bf16[15,128,256]{2,1,0:T(8,128)(2,1)S(1)}, bf16[15,128,256]{2,1,0:T(8,128)(2,1)S(1)}, u32[]{:S(2)}, u32[]{:S(2)}) collective-permute-start(bf16[15,128,256]{2,1,0:T(8,128)(2,1)S(1)} %collective-permute-done), channel_id=1, source_target_pairs={{0,1},{1,2},{2,3},{3,4},{4,5},{5,6},{6,7},{7,0},{8,9},{9,10},{10,1... | collective-permute-start | bytes 2949128 | tf_op jit(solution)/shard_map/ppermute | solution.py:24
  35.9 26.1 %collective-permute-start.4 = (bf16[15,128,256]{2,1,0:T(8,128)(2,1)}, bf16[15,128,256]{2,1,0:T(8,128)(2,1)}, u32[]{:S(2)}, u32[]{:S(2)}) collective-permute-start(bf16[15,128,256]{2,1,0:T(8,128)(2,1)} %param.9), channel_id=1, source_target_pairs={{1,0},{2,1},{3,2},{4,3},{5,4},{6,5},{7,6},{0,7},{9,8},{10,9},{11,1... | collective-permute-start | bytes 2949128 | tf_op jit(solution)/shard_map/ppermute | solution.py:26
  59.1 1.0 copy-start.3
  60.1 24.4 %collective-permute-start.2 = (bf16[15,128,256]{2,1,0:T(8,128)(2,1)S(1)}, bf16[15,128,256]{2,1,0:T(8,128)(2,1)}, u32[]{:S(2)}, u32[]{:S(2)}) collective-permute-start(bf16[15,128,256]{2,1,0:T(8,128)(2,1)S(1)} %collective-permute-done.1), channel_id=1, source_target_pairs={{0,1},{1,2},{2,3},{3,4},{4,5},{5,6},{6,7},{7,0},{8,9},{9,10},{10,1... | collective-permute-start | bytes 2949128 | tf_op jit(solution)/shard_map/ppermute | solution.py:24
  62.0 25.4 %collective-permute-start.5 = (bf16[15,128,256]{2,1,0:T(8,128)(2,1)}, bf16[15,128,256]{2,1,0:T(8,128)(2,1)}, u32[]{:S(2)}, u32[]{:S(2)}) collective-permute-start(bf16[15,128,256]{2,1,0:T(8,128)(2,1)} %collective-permute-done.4), channel_id=1, source_target_pairs={{1,0},{2,1},{3,2},{4,3},{5,4},{6,5},{7,6},{0,7},{9,8},{10,9},{11,1... | collective-permute-start | bytes 2949128 | tf_op jit(solution)/shard_map/ppermute | solution.py:26
  84.5 23.8 %collective-permute-start.3 = (bf16[15,128,256]{2,1,0:T(8,128)(2,1)}, bf16[15,128,256]{2,1,0:T(8,128)(2,1)}, u32[]{:S(2)}, u32[]{:S(2)}) collective-permute-start(bf16[15,128,256]{2,1,0:T(8,128)(2,1)} %collective-permute-done.2), channel_id=1, source_target_pairs={{0,1},{1,2},{2,3},{3,4},{4,5},{5,6},{6,7},{7,0},{8,9},{9,10},{10,1... | collective-permute-start | bytes 2949128 | tf_op jit(solution)/shard_map/ppermute | solution.py:24
  87.4 34.2 %collective-permute-start.6 = (bf16[15,128,256]{2,1,0:T(8,128)(2,1)}, bf16[15,128,256]{2,1,0:T(8,128)(2,1)S(1)}, u32[]{:S(2)}, u32[]{:S(2)}) collective-permute-start(bf16[15,128,256]{2,1,0:T(8,128)(2,1)} %collective-permute-done.5), channel_id=1, source_target_pairs={{1,0},{2,1},{3,2},{4,3},{5,4},{6,5},{7,6},{0,7},{9,8},{10,9},{11,1... | collective-permute-start | bytes 2949128 | tf_op jit(solution)/shard_map/ppermute | solution.py:26
  130.4 10.7 %copy-start.1 = (bf16[15,128,256]{2,1,0:T(8,128)(2,1)S(1)}, bf16[15,128,256]{2,1,0:T(8,128)(2,1)}, u32[]{:S(2)}) copy-start(bf16[15,128,256]{2,1,0:T(8,128)(2,1)} %param.8) | copy-start | bytes 2949124
  148.0 18.7 %copy-start.4 = (s32[960]{0:T(1024)S(1)}, s32[960]{0:T(1024)}, u32[]{:S(2)}) copy-start(s32[960]{0:T(1024)} %param.14) | copy-start | bytes 11524
  148.0 18.7 %copy-start.5 = (s32[960]{0:T(1024)S(1)}, s32[960]{0:T(1024)}, u32[]{:S(2)}) copy-start(s32[960]{0:T(1024)} %param.13) | copy-start | bytes 11524
  148.0 116.5 %copy-start.7 = (f32[256,8]{0,1:T(8,128)S(1)}, f32[256,8]{0,1:T(8,128)}, u32[]{:S(2)}) copy-start(f32[256,8]{0,1:T(8,128)} %param.12) | copy-start | bytes 24580
  148.0 116.5 %copy-start.8 = (f32[256]{0:T(256)S(1)}, f32[256]{0:T(256)}, u32[]{:S(2)}) copy-start(f32[256]{0:T(256)} %param.11) | copy-start | bytes 3076
  152.4 117.2 %copy-start.6 = (s32[384]{0:T(512)S(1)}, s32[384]{0:T(512)}, u32[]{:S(2)}) copy-start(s32[384]{0:T(512)} %param.15) | copy-start | bytes 4612
  152.4 109.0 %all-to-all-start = ((bf16[64,128,256]{2,1,0:T(8,128)(2,1)}), bf16[64,128,256]{2,1,0:T(8,128)(2,1)}, u32[]{:S(2)}, u32[]{:S(2)}) async-start(bf16[64,128,256]{2,1,0:T(8,128)(2,1)} %copy.41), calls=%async_computation | async-start | bytes 8388608 | tf_op jit(solution)/shard_map/all_to_all | solution.py:108
  266.2 15.2 %all-to-all-start.1 = ((f32[8,1,11520]{2,1,0:T(1,128)}), f32[8,1,11520]{2,1,0:T(1,128)S(1)}, u32[]{:S(2)}, u32[]{:S(2)}) async-start(f32[8,1,11520]{2,1,0:T(1,128)} %broadcast_in_dim.90), calls=%async_computation.1 | async-start | bytes 737280 | tf_op jit(solution)/shard_map/all_to_all | solution.py:35
  283.4 22.6 %all-to-all-start.2 = ((f32[64,6,8]{2,1,0:T(8,128)}), f32[64,6,8]{2,1,0:T(8,128)S(1)}, u32[]{:S(2)}, u32[]{:S(2)}) async-start(f32[64,6,8]{2,1,0:T(8,128)} %copy.44), calls=%async_computation.2 | async-start | bytes 524288 | tf_op jit(solution)/shard_map/all_to_all | solution.py:58
